TPU v7x, 32 devices: a whole 2x2x4 slice. The times are simulated.
32 devices in a mesh: row: 8 (over z, core), col: 4 (over y, x).
Axes of the slice: x: 2, y: 2, z: 4, core: 2. Of those that a mesh axis runs over, the one named last changes fastest.
Arguments:
- x_fwd: bfloat16 [512, 6144], P('row', 'col'), may hold values from -6 to 6
- x_bwd: bfloat16 [512, 6144], P('row', 'col'), may hold values from -6 to 6
- grad_out: bfloat16 [512, 6144], P('row', 'col'), may hold values from -1.5 to 1.5
- gain: float32 [6144], P('col'), may hold values from 0.1 to 1.9
- w_up: bfloat16 [6144, 12288], P('col', 'row'), may hold values from -0.078125 to 0.078125
- w_down: bfloat16 [12288, 6144], P('row', 'col'), may hold values from -0.0546875 to 0.0546875
Outputs:
- y_fwd: bfloat16 [512, 6144], P('row', 'col')
- dx_bwd: bfloat16 [512, 6144], P('row', 'col')
- step_up: float32 [6144, 12288], P('col', 'row')
- step_down: float32 [12288, 6144], P('row', 'col')
- step_gain: float32 [6144], P('col')
- grad_rms: float32 [], replicated
All inputs are finite; a program needn't handle non-finite values.
Results may differ from a plain program's by a relative error of at most 0.0017.
The roundings to bfloat16 on the way count: a program that leaves them out, or rounds other values in their place, can miss the bound.
Values may be sent and summed in bfloat16 or wider, within the bound.
A program may use at most 128 MiB of HBM per device.

v0:
```python
import math
import jax
import jax.numpy as jnp
from jax import lax
from jax.sharding import PartitionSpec as P

D = 6144
FF = 12288
eps = 1e-06
clip_share = 0.25


def erf_gelu(value):
    return 0.5 * value * (1.0 + lax.erf(value * 0.7071067811865476))


def gelu_slope(value):
    return (
        0.5 * (1.0 + lax.erf(value * 0.7071067811865476))
        + value * jnp.exp(-0.5 * value * value) * 0.3989422804014327
    )


def contract(left, right, left_dim, right_dim):
    return lax.dot_general(
        left, right, (((left_dim,), (right_dim,)), ((), ())), preferred_element_type=jnp.float32
    )


def row_sums(tokens):
    values = tokens.astype(jnp.float32)
    return (jnp.sum(values, -1), jnp.sum(values * values, -1))


def normalize(tokens, first, second):
    values = tokens.astype(jnp.float32)
    centre = first / D
    spread = second / D - centre * centre
    inv_scale = lax.rsqrt(spread + eps)
    return ((values - centre[:, None]) * inv_scale[:, None], inv_scale)


def up_both(normed_a, normed_b, w_up):
    full_a, full_b = (
        lax.all_gather(normed_a, "row", axis=0, tiled=True),
        lax.all_gather(normed_b, "row", axis=0, tiled=True),
    )
    width = w_up.shape[1]
    summed = lax.psum_scatter(
        jnp.concatenate(
            [
                jnp.dot(full_a, w_up, preferred_element_type=jnp.float32),
                jnp.dot(full_b, w_up, preferred_element_type=jnp.float32),
            ],
            1,
        ),
        "col",
        scatter_dimension=0,
        tiled=True,
    )
    return (summed[:, :width], summed[:, width:], full_b)


def on_device(x_fwd, x_bwd, grad_out, gain, w_up, w_down):
    first_a, second_a = row_sums(x_fwd)
    first_b, second_b = row_sums(x_bwd)
    first_a, second_a, first_b, second_b = lax.psum((first_a, second_a, first_b, second_b), "col")
    centred_a, _ = normalize(x_fwd, first_a, second_a)
    centred_b, inv_scale = normalize(x_bwd, first_b, second_b)
    normed_a = (centred_a * gain).astype(jnp.bfloat16)
    normed_b = (centred_b * gain).astype(jnp.bfloat16)
    pre_a, pre_b, normed_full = up_both(normed_a, normed_b, w_up)
    hidden_a = erf_gelu(pre_a).astype(jnp.bfloat16)
    output_part = jnp.dot(
        lax.all_gather(hidden_a, "col", axis=0, tiled=True),
        w_down,
        preferred_element_type=jnp.float32,
    )
    output_sum = lax.psum_scatter(output_part, "row", scatter_dimension=0, tiled=True)
    y_fwd = (x_fwd.astype(jnp.float32) + output_sum).astype(jnp.bfloat16)
    hidden_b = erf_gelu(pre_b).astype(jnp.bfloat16)
    grad_full = lax.all_gather(grad_out, "row", axis=0, tiled=True)
    grad_hidden = lax.psum_scatter(
        contract(grad_full, w_down, 1, 1), "col", scatter_dimension=0, tiled=True
    )
    grad_pre = (grad_hidden * gelu_slope(pre_b)).astype(jnp.bfloat16)
    hidden_piece = lax.all_gather(hidden_b, "col", axis=0, tiled=True)
    pre_piece = lax.all_gather(grad_pre, "col", axis=0, tiled=True)
    down_total = contract(hidden_piece, grad_full, 0, 0)
    up_total = contract(normed_full, pre_piece, 0, 0)
    input_total = contract(pre_piece, w_up, 1, 1)
    grad_normed = lax.psum_scatter(input_total, "row", scatter_dimension=0, tiled=True)
    scaled = grad_normed * gain
    first_back = jnp.sum(scaled, -1)
    second_back = jnp.sum(scaled * centred_b, -1)
    first_back, second_back = lax.psum((first_back, second_back), "col")
    dx_bwd = (
        grad_out.astype(jnp.float32)
        + inv_scale[:, None]
        * (scaled - first_back[:, None] / D - centred_b * (second_back[:, None] / D))
    ).astype(jnp.bfloat16)
    gain_part = jnp.sum(grad_normed * centred_b, 0)
    weight_squares = jnp.sum(up_total * up_total) + jnp.sum(down_total * down_total)
    g_gain = lax.psum(gain_part, "row")
    first_row = (lax.axis_index("row") == 0).astype(jnp.float32)
    total = lax.psum(weight_squares + first_row * jnp.sum(g_gain * g_gain), ("row", "col"))
    param_count = 2 * D * FF + D
    norm_value = jnp.sqrt(total)
    grad_rms = norm_value / math.sqrt(param_count)
    factor = jnp.minimum(1.0, clip_share * math.sqrt(param_count) / norm_value)
    return (y_fwd, dx_bwd, up_total * factor, down_total * factor, g_gain * factor, grad_rms)


def solution(mesh):
    placed = (
        P("row", "col"),
        P("row", "col"),
        P("row", "col"),
        P("col"),
        P("col", "row"),
        P("row", "col"),
    )
    return jax.shard_map(
        on_device,
        mesh=mesh,
        in_specs=placed,
        out_specs=(
            P("row", "col"),
            P("row", "col"),
            P("col", "row"),
            P("row", "col"),
            P("col"),
            P(),
        ),
        check_vma=False,
    )
```

profile of v0, /device:TPU:0, one launch (start us, length us, event | category | flops | bytes accessed | tf_op | source)
XLA Modules:
  0.0 446.6 jit_solution(12459251885347289089)
XLA Ops:
  7.2 0.0 all-gather.13.cloned.1.call-start
  7.2 0.7 all-gather.13.cloned.1.call-update
  7.9 0.0 all-gather.7.cloned.1.call-start
  7.9 1.1 convert_reduce_fusion
  9.0 1.1 convert_reduce_fusion.1
  10.1 11.4 %all-reduce.1 = (f32[64]{0:T(128)S(1)}, f32[64]{0:T(128)S(1)}, f32[64]{0:T(128)S(1)}, f32[64]{0:T(128)S(1)}) all-reduce(f32[64]{0:T(128)S(1)} %get-tuple-element.12, f32[64]{0:T(128)S(1)} %get-tuple-element.11, f32[64]{0:T(128)S(1)} %get-tuple-element.10, f32[64]{0:T(128)S(1)} %get-tuple-element.9), channel_id=1, replica_groups=mesh['row'=8,'col'=4] {'col'}, use_global_device_ids=true, to_apply=%region_7.0 | all-reduce | flops 256 | bytes 2048 | tf_op jit(solution)/shard_map/psum | solution.py:67
  21.5 2.0 fusion.21
  23.6 0.0 all-gather.9.cloned.1.call-start
  23.6 0.7 all-gather.9.cloned.1.call-update
  24.3 0.0 reduce-scatter.9.cloned.1.call-start
  24.4 13.3 %all-gather.13.cloned.1.call-done = bf16[512,1536]{1,0:T(8,128)(2,1)} async-done(((bf16[64,1536]{1,0:T(8,128)(2,1)}), bf16[512,1536]{1,0:T(8,128)(2,1)}) %all-gather.13.cloned.1.call-update) | async-done | bytes 1572880 | tf_op jit(solution)/shard_map/all_gather | solution.py:82
  37.6 7.1 %fusion.27 = f32[512,1536]{1,0:T(8,128)} fusion(bf16[512,1536]{1,0:T(8,128)(2,1)} %all-gather.13.cloned.1.call-done, bf16[1536,1536]{1,0:T(8,128)(2,1)} %param.11), kind=kOutput, calls=%fused_computation.52 | convolution fusion | flops 2415919104 | bytes 9437184 | tf_op jit(solution)/shard_map/dot_general | solution.py:25
  44.8 0.0 reduce-scatter.5.cloned.1.call-start
  44.8 19.4 %all-gather.7.cloned.1.call-done = bf16[512,1536]{1,0:T(8,128)(2,1)} async-done(((bf16[64,1536]{1,0:T(8,128)(2,1)}), bf16[512,1536]{1,0:T(8,128)(2,1)}) %all-gather.7.cloned.1.call-update) | async-done | bytes 1572880 | tf_op jit(solution)/shard_map/all_gather | solution.py:45
  64.3 4.9 %fusion.24 = f32[512,1536]{1,0:T(8,128)S(1)} fusion(bf16[512,1536]{1,0:T(8,128)(2,1)} %all-gather.7.cloned.1.call-done, bf16[1536,1536]{1,0:T(8,128)(2,1)} %param.10), kind=kOutput, calls=%fused_computation.49 | convolution fusion | flops 2415919104 | bytes 9437184 | tf_op jit(solution)/shard_map/dot_general | solution.py:52
  69.2 21.7 %all-gather.9.cloned.1.call-done = bf16[512,1536]{1,0:T(8,128)(2,1)} async-done(((bf16[64,1536]{1,0:T(8,128)(2,1)}), bf16[512,1536]{1,0:T(8,128)(2,1)}) %all-gather.9.cloned.1.call-update) | async-done | bytes 1572880 | tf_op jit(solution)/shard_map/all_gather | solution.py:46
  90.9 4.9 %fusion.25 = f32[512,1536]{1,0:T(8,128)S(1)} fusion(bf16[512,1536]{1,0:T(8,128)(2,1)} %all-gather.9.cloned.1.call-done, bf16[1536,1536]{1,0:T(8,128)(2,1)} %param.10), kind=kOutput, calls=%fused_computation.50 | convolution fusion | flops 2415919104 | bytes 9437184 | tf_op jit(solution)/shard_map/dot_general | solution.py:53
  95.9 3.3 pad_maximum_fusion
  99.1 0.0 all-gather.15.cloned.1.call-start
  99.2 38.2 %reduce-scatter.9.cloned.1.call-done = f32[128,1536]{1,0:T(8,128)} async-done(((f32[512,1536]{1,0:T(8,128)}), f32[128,1536]{1,0:T(8,128)}) %reduce-scatter.9.cloned.1.call-update) | async-done | bytes 786448 | tf_op jit(solution)/shard_map/reduce_scatter | solution.py:83
  137.4 73.5 %reduce-scatter.5.cloned.1.call-done = f32[128,3072]{1,0:T(8,128)} async-done(((f32[512,3072]{1,0:T(8,128)}), f32[128,3072]{1,0:T(8,128)}) %reduce-scatter.5.cloned.1.call-update) | async-done | bytes 1572880 | tf_op jit(solution)/shard_map/reduce_scatter | solution.py:49
  210.9 3.0 multiply_convert_fusion
  213.9 0.0 all-gather.11.cloned.1.call-start
  214.0 0.7 all-gather.11.cloned.1.call-update
  214.7 0.0 all-gather.17.cloned.1.call-start
  214.7 0.7 all-gather.17.cloned.1.call-update
  215.4 0.0 reduce-scatter.11.cloned.1.call-start
  215.5 29.5 %all-gather.15.cloned.1.call-done = bf16[512,1536]{1,0:T(8,128)(2,1)} async-done(((bf16[128,1536]{1,0:T(8,128)(2,1)}), bf16[512,1536]{1,0:T(8,128)(2,1)}) %all-gather.15.cloned.1.call-update) | async-done | bytes 1572880 | tf_op jit(solution)/shard_map/all_gather | solution.py:88
  244.9 7.1 %fusion.28 = f32[512,1536]{1,0:T(8,128)} fusion(bf16[512,1536]{1,0:T(8,128)(2,1)} %all-gather.15.cloned.1.call-done, bf16[1536,1536]{1,0:T(8,128)(2,1)} %param.10), kind=kOutput, calls=%fused_computation.53 | convolution fusion | flops 2415919104 | bytes 9437184 | tf_op jit(solution)/shard_map/dot_general | solution.py:25
  252.1 0.2 reduce-scatter.7.cloned.1.call-start
  252.3 25.3 %all-gather.11.cloned.1.call-done = bf16[512,1536]{1,0:T(8,128)(2,1)} async-done(((bf16[128,1536]{1,0:T(8,128)(2,1)}), bf16[512,1536]{1,0:T(8,128)(2,1)}) %all-gather.11.cloned.1.call-update) | async-done | bytes 1572880 | tf_op jit(solution)/shard_map/all_gather | solution.py:75
  277.6 7.1 %fusion.26 = f32[512,1536]{1,0:T(8,128)} fusion(bf16[512,1536]{1,0:T(8,128)(2,1)} %all-gather.11.cloned.1.call-done, bf16[1536,1536]{1,0:T(8,128)(2,1)} %param.11), kind=kOutput, calls=%fused_computation.51 | convolution fusion | flops 2415919104 | bytes 9437184 | tf_op jit(solution)/shard_map/dot_general | solution.py:74
  284.8 1.4 copy-done.5
  286.2 0.5 copy-done.6
  286.7 6.0 %multiply_reduce_fusion.1 = (f32[]{:T(128)}, f32[1536,1536]{1,0:T(8,128)}) fusion(bf16[512,1536]{1,0:T(8,128)(2,1)S(1)} %copy-done.5, bf16[512,1536]{1,0:T(8,128)(2,1)S(1)} %copy-done.6), kind=kOutput, calls=%fused_computation.1 | convolution fusion | flops 2420637696 | bytes 12582916 | tf_op jit(solution)/shard_map/dot_general | solution.py:25
  292.7 18.2 %all-gather.17.cloned.1.call-done = bf16[512,1536]{1,0:T(8,128)(2,1)} async-done(((bf16[128,1536]{1,0:T(8,128)(2,1)}), bf16[512,1536]{1,0:T(8,128)(2,1)}) %all-gather.17.cloned.1.call-update) | async-done | bytes 1572880 | tf_op jit(solution)/shard_map/all_gather | solution.py:87
  310.9 8.9 %multiply_reduce_fusion = (f32[]{:T(128)}, f32[1536,1536]{1,0:T(8,128)}) fusion(bf16[512,1536]{1,0:T(8,128)(2,1)} %all-gather.17.cloned.1.call-done, bf16[512,1536]{1,0:T(8,128)(2,1)} %all-gather.13.cloned.1.call-done), kind=kOutput, calls=%fused_computation | convolution fusion | flops 2420637696 | bytes 12582916 | tf_op jit(solution)/shard_map/dot_general | solution.py:25
  321.1 32.5 %reduce-scatter.11.cloned.1.call-done = f32[64,1536]{1,0:T(8,128)} async-done(((f32[512,1536]{1,0:T(8,128)}), f32[64,1536]{1,0:T(8,128)}) %reduce-scatter.11.cloned.1.call-update) | async-done | bytes 393232 | tf_op jit(solution)/shard_map/reduce_scatter | solution.py:92
  353.6 1.4 fusion.17
  355.0 16.1 %psum.62 = f32[1536]{0:T(1024)S(1)} all-reduce(f32[1536]{0:T(1024)S(1)} %get-tuple-element.6), channel_id=1, replica_groups=mesh['row'=8,'col'=4] {'row'}, use_global_device_ids=true, to_apply=%region_19.0 | all-reduce | flops 1536 | bytes 12288 | tf_op jit(solution)/shard_map/psum | solution.py:104
  371.1 0.6 multiply_reduce_fusion.3
  372.3 38.8 %psum.63 = f32[]{:T(128)} all-reduce(f32[]{:T(128)S(6)} %add.60), channel_id=1, replica_groups=mesh['row'=8,'col'=4] {'row','col'}, use_global_device_ids=true, to_apply=%region_21.0 | all-reduce | flops 1 | bytes 8 | tf_op jit(solution)/shard_map/psum | solution.py:106
  411.9 9.9 %all-reduce = (f32[64]{0:T(128)S(1)}, f32[64]{0:T(128)S(1)}) all-reduce(f32[64]{0:T(128)S(1)} %get-tuple-element.7, f32[64]{0:T(128)S(1)} %get-tuple-element.8), channel_id=1, replica_groups=mesh['row'=8,'col'=4] {'col'}, use_global_device_ids=true, to_apply=%region_15.0 | all-reduce | flops 128 | bytes 1024 | tf_op jit(solution)/shard_map/psum | solution.py:96
  421.8 0.6 broadcast_multiply_fusion.2
  422.5 8.7 %broadcast_multiply_fusion = f32[1536,1536]{1,0:T(8,128)} fusion(f32[1536,1536]{1,0:T(8,128)} %get-tuple-element.31, f32[]{:T(128)S(6)} %min.3), kind=kLoop, calls=%fused_computation.3 | loop fusion | flops 2359296 | bytes 18874372 | tf_op jit(solution)/shard_map/mul | solution.py:111
  431.2 4.8 %broadcast_multiply_fusion.1 = f32[1536,1536]{1,0:T(8,128)} fusion(f32[1536,1536]{1,0:T(8,128)S(1)} %bitcast.15, f32[]{:T(128)S(6)} %min.3), kind=kLoop, calls=%fused_computation.4 | loop fusion | flops 2359296 | bytes 18874372 | tf_op jit(solution)/shard_map/mul | solution.py:111
  436.0 1.7 fusion.23
  437.7 0.9 fusion.16
  (29 shorter events, 0.2 us)
Async XLA Ops:
  7.2 30.5 %all-gather.13.cloned.1.call-start = ((), (), s32[]{:S(2)}) async-start(), calls=%async_computation.9 | async-start | bytes 1769472 | tf_op jit(solution)/shard_map/all_gather | solution.py:82
  7.9 56.4 %all-gather.7.cloned.1.call-start = ((), (), s32[]{:S(2)}) async-start(), calls=%async_computation.4 | async-start | bytes 1769472 | tf_op jit(solution)/shard_map/all_gather | solution.py:45
  23.6 67.3 %all-gather.9.cloned.1.call-start = ((), (), s32[]{:S(2)}) async-start(), calls=%async_computation.5 | async-start | bytes 1769472 | tf_op jit(solution)/shard_map/all_gather | solution.py:46
  24.3 113.1 %reduce-scatter.9.cloned.1.call-start = ((), (), s32[]{:S(2)}) async-start(), calls=%async_computation.10 | async-start | bytes 3932160 | tf_op jit(solution)/shard_map/reduce_scatter | solution.py:83
  44.8 166.1 %reduce-scatter.5.cloned.1.call-start = ((), (), s32[]{:S(2)}) async-start(), calls=%async_computation.6 | async-start | bytes 7864320 | tf_op jit(solution)/shard_map/reduce_scatter | solution.py:49
  99.1 145.8 %all-gather.15.cloned.1.call-start = ((), (), s32[]{:S(2)}) async-start(), calls=%async_computation.11 | async-start | bytes 1966080 | tf_op jit(solution)/shard_map/all_gather | solution.py:88
  213.9 63.7 %all-gather.11.cloned.1.call-start = ((), (), s32[]{:S(2)}) async-start(), calls=%async_computation.7 | async-start | bytes 1966080 | tf_op jit(solution)/shard_map/all_gather | solution.py:75
  214.7 96.2 %all-gather.17.cloned.1.call-start = ((), (), s32[]{:S(2)}) async-start(), calls=%async_computation.13 | async-start | bytes 1966080 | tf_op jit(solution)/shard_map/all_gather | solution.py:87
  215.4 138.2 %reduce-scatter.11.cloned.1.call-start = ((), (), s32[]{:S(2)}) async-start(), calls=%async_computation.12 | async-start | bytes 3538944 | tf_op jit(solution)/shard_map/reduce_scatter | solution.py:92
  252.1 183.9 %reduce-scatter.7.cloned.1.call-start = ((), (), s32[]{:S(2)}) async-start(), calls=%async_computation.8 | async-start | bytes 3538944 | tf_op jit(solution)/shard_map/reduce_scatter | solution.py:79
  284.8 1.4 copy-start.5
  284.8 1.9 copy-start.6
  292.7 60.9 %copy-start = (bf16[64,1536]{1,0:T(8,128)(2,1)S(1)}, bf16[64,1536]{1,0:T(8,128)(2,1)}, u32[]{:S(2)}) copy-start(bf16[64,1536]{1,0:T(8,128)(2,1)} %param.7) | copy-start | bytes 589828
  292.7 60.9 %copy-start.4 = (f32[1536]{0:T(1024)S(1)}, f32[1536]{0:T(1024)}, u32[]{:S(2)}) copy-start(f32[1536]{0:T(1024)} %param.9) | copy-start | bytes 18436
  353.6 77.5 %slice-start = ((s8[9437184]{0:T(1024)(128)(4,1)}), s8[1048576]{0:T(1024)(128)(4,1)S(1)}, s32[]{:S(2)}) async-start(s8[9437184]{0:T(1024)(128)(4,1)} %bitcast.14), calls=%async_computation.14 | async-start | bytes 2097152
  422.4 8.7 %slice-start.1 = ((s8[9437184]{0:T(1024)(128)(4,1)}), s8[4194304]{0:T(1024)(128)(4,1)S(1)}, s32[]{:S(2)}) async-start(s8[9437184]{0:T(1024)(128)(4,1)} %bitcast.14), calls=%async_computation.15 | async-start | bytes 8388608
  422.4 8.7 %slice-start.2 = ((s8[9437184]{0:T(1024)(128)(4,1)}), s8[4194304]{0:T(1024)(128)(4,1)S(1)}, s32[]{:S(2)}) async-start(s8[9437184]{0:T(1024)(128)(4,1)} %bitcast.14), calls=%async_computation.16 | async-start | bytes 8388608
  431.1 4.8 %copy-start.1 = (bf16[64,1536]{1,0:T(8,128)(2,1)S(1)}, bf16[64,1536]{1,0:T(8,128)(2,1)}, u32[]{:S(2)}) copy-start(bf16[64,1536]{1,0:T(8,128)(2,1)} %param.6) | copy-start | bytes 589828
  431.2 6.5 %copy-start.2 = (f32[64,1536]{1,0:T(8,128)S(1)}, f32[64,1536]{1,0:T(8,128)}, u32[]{:S(2)}) copy-start(f32[64,1536]{1,0:T(8,128)} %reduce-scatter.11.cloned.1.call-done) | copy-start | bytes 1179652
  431.2 6.5 %copy-start.3 = (bf16[64,1536]{1,0:T(8,128)(2,1)S(1)}, bf16[64,1536]{1,0:T(8,128)(2,1)}, u32[]{:S(2)}) copy-start(bf16[64,1536]{1,0:T(8,128)(2,1)} %param.8) | copy-start | bytes 589828
Sparse Core Ops, SparseCore 0:
  9.6 27.9 all-gather.12
  39.8 24.3 all-gather.6
  66.5 24.3 all-gather.8
  94.3 43.0 reduce-scatter.8
  140.8 70.0 reduce-scatter.4
  214.0 30.8 all-gather.14
  246.8 30.8 all-gather.10
  280.0 30.8 all-gather.16
  313.2 40.3 reduce-scatter.10
  355.8 40.2 reduce-scatter.6
where the time goes:
time: 447 us
  waiting for transfers between devices  274 us (61%)
  blocking collectives  76.2 us (17%)
  matrix products  46.1 us (10%)
  other arithmetic  29.2 us (7%)
  between operations  18.1 us (4%)
    reduce_scatter x1, waiting for transfers between devices, up_both(): lax.psum_scatter(jnp.concatenate([jnp.dot(full_a, w_up, preferred_element...  73.5 us
    psum x1, blocking collectives, on_device(): lax.psum(weight_squares + first_row * jnp.sum(g_gain * g_gain), ('row', '...  38.8 us
    reduce_scatter x1, waiting for transfers between devices, on_device(): lax.psum_scatter(contract(grad_full, w_down, 1, 1), 'col', scatter_dimens...  38.2 us
    reduce_scatter x1, waiting for transfers between devices, on_device(): lax.psum_scatter(input_total, 'row', scatter_dimension=0, tiled=True)  32.5 us
    all_gather x1, waiting for transfers between devices, on_device(): pre_piece = lax.all_gather(grad_pre, 'col', axis=0, tiled=True)  29.5 us
    dot_general x4, matrix products, contract(): lax.dot_general(left, right, (((left_dim,), (right_dim,)), ((), ())), pre...  29.2 us
    all_gather x1, waiting for transfers between devices, on_device(): lax.all_gather(hidden_a, 'col', axis=0, tiled=True)  25.3 us
    all_gather x1, waiting for transfers between devices, up_both(): lax.all_gather(normed_b, 'row', axis=0, tiled=True)  21.7 us
  transfers between devices with their start and end apart: 10, of which 9 were waited for; matrix products, arithmetic and copies ran while one was open for 16% of the time, Pallas kernels for 0%

commit v1 on v0

--- a/solution.py
+++ b/solution.py
@@ -84,8 +84,11 @@
         contract(grad_full, w_down, 1, 1), "col", scatter_dimension=0, tiled=True
     )
     grad_pre = (grad_hidden * gelu_slope(pre_b)).astype(jnp.bfloat16)
-    hidden_piece = lax.all_gather(hidden_b, "col", axis=0, tiled=True)
-    pre_piece = lax.all_gather(grad_pre, "col", axis=0, tiled=True)
+    hidden_piece, pre_piece = jnp.split(
+        lax.all_gather(jnp.concatenate([hidden_b, grad_pre], axis=1), "col", axis=0, tiled=True),
+        [hidden_b.shape[1]],
+        axis=1,
+    )
     down_total = contract(hidden_piece, grad_full, 0, 0)
     up_total = contract(normed_full, pre_piece, 0, 0)
     input_total = contract(pre_piece, w_up, 1, 1)

time: 447 us -> 465 us (1.040)
  waiting for transfers between devices: 274 us -> 295 us
    reduce_scatter x1, waiting for transfers between devices: 0.01 us -> 18.1 us  [on_device(): lax.psum_scatter(output_part, 'row', scatter_dimension=0, tiled=True)]
    all_gather x2 -> x1, waiting for transfers between devices: 47.6 us -> 38.9 us  [on_device(): lax.all_gather(jnp.concatenate([hidden_b, grad_pre], axis=1), 'col', axis...]
    reduce_scatter x1, waiting for transfers between devices: 32.5 us -> 40.3 us  [on_device(): lax.psum_scatter(input_total, 'row', scatter_dimension=0, tiled=True)]
  transfers between devices with their start and end apart: 10 -> 9, of which waited for: 9 -> 9; matrix products, arithmetic and copies ran while one was open for 16% -> 12% of each run, Pallas kernels for 0% -> 0%
where the time goes in v1:
time: 465 us; the launch traced here: 464 us
  waiting for transfers between devices  295 us (63%)
  blocking collectives  73.5 us (16%)
  matrix products  45.1 us (10%)
  other arithmetic  30 us (6%)
  between operations  17.8 us (4%)
    reduce_scatter x1, waiting for transfers between devices, up_both(): lax.psum_scatter(jnp.concatenate([jnp.dot(full_a, w_up, preferred_element...  73.5 us
    reduce_scatter x1, waiting for transfers between devices, on_device(): lax.psum_scatter(input_total, 'row', scatter_dimension=0, tiled=True)  40.3 us
    all_gather x1, waiting for transfers between devices, on_device(): lax.all_gather(jnp.concatenate([hidden_b, grad_pre], axis=1), 'col', axis...  38.9 us
    reduce_scatter x1, waiting for transfers between devices, on_device(): lax.psum_scatter(contract(grad_full, w_down, 1, 1), 'col', scatter_dimens...  38.2 us
    psum x1, blocking collectives, on_device(): lax.psum(weight_squares + first_row * jnp.sum(g_gain * g_gain), ('row', '...  36.9 us
    all_gather x1, waiting for transfers between devices, on_device(): lax.all_gather(hidden_a, 'col', axis=0, tiled=True)  29.9 us
    dot_general x4, matrix products, contract(): lax.dot_general(left, right, (((left_dim,), (right_dim,)), ((), ())), pre...  28.2 us
    all_gather x1, waiting for transfers between devices, up_both(): lax.all_gather(normed_b, 'row', axis=0, tiled=True)  21.7 us
  transfers between devices with their start and end apart: 9, of which 9 were waited for; matrix products, arithmetic and copies ran while one was open for 12% of the time, Pallas kernels for 0%

profile of v1, /device:TPU:0, one launch (start us, length us, event | category | flops | bytes accessed | tf_op | source)
XLA Modules:
  0.0 464.0 jit_solution(17538693833433128261)
XLA Ops:
  7.2 0.0 all-gather.12.cloned.1.call-start
  7.2 0.7 all-gather.12.cloned.1.call-update
  7.9 0.0 all-gather.6.cloned.1.call-start
  7.9 1.1 convert_reduce_fusion
  9.0 1.1 convert_reduce_fusion.1
  10.1 11.4 %all-reduce.1 = (f32[64]{0:T(128)S(1)}, f32[64]{0:T(128)S(1)}, f32[64]{0:T(128)S(1)}, f32[64]{0:T(128)S(1)}) all-reduce(f32[64]{0:T(128)S(1)} %get-tuple-element.12, f32[64]{0:T(128)S(1)} %get-tuple-element.11, f32[64]{0:T(128)S(1)} %get-tuple-element.10, f32[64]{0:T(128)S(1)} %get-tuple-element.9), channel_id=1, replica_groups=mesh['row'=8,'col'=4] {'col'}, use_global_device_ids=true, to_apply=%region_7.0 | all-reduce | flops 256 | bytes 2048 | tf_op jit(solution)/shard_map/psum | solution.py:67
  21.5 2.0 fusion.27
  23.6 0.0 all-gather.6.cloned.1.call-update
  23.6 0.0 all-gather.8.cloned.1.call-start
  23.6 0.7 all-gather.8.cloned.1.call-update
  24.3 0.0 reduce-scatter.9.cloned.1.call-start
  24.4 13.3 %all-gather.12.cloned.1.call-done = bf16[512,1536]{1,0:T(8,128)(2,1)} async-done(((bf16[64,1536]{1,0:T(8,128)(2,1)}), bf16[512,1536]{1,0:T(8,128)(2,1)}) %all-gather.12.cloned.1.call-update) | async-done | bytes 1572880 | tf_op jit(solution)/shard_map/all_gather | solution.py:82
  37.6 7.1 %fusion.33 = f32[512,1536]{1,0:T(8,128)} fusion(bf16[512,1536]{1,0:T(8,128)(2,1)} %all-gather.12.cloned.1.call-done, bf16[1536,1536]{1,0:T(8,128)(2,1)} %param.11), kind=kOutput, calls=%fused_computation.59 | convolution fusion | flops 2415919104 | bytes 9437184 | tf_op jit(solution)/shard_map/dot_general | solution.py:25
  44.8 0.0 reduce-scatter.9.cloned.1.call-update
  44.8 0.0 reduce-scatter.5.cloned.1.call-start
  44.8 19.4 %all-gather.6.cloned.1.call-done = bf16[512,1536]{1,0:T(8,128)(2,1)} async-done(((bf16[64,1536]{1,0:T(8,128)(2,1)}), bf16[512,1536]{1,0:T(8,128)(2,1)}) %all-gather.6.cloned.1.call-update) | async-done | bytes 1572880 | tf_op jit(solution)/shard_map/all_gather | solution.py:45
  64.3 4.9 %fusion.30 = f32[512,1536]{1,0:T(8,128)S(1)} fusion(bf16[512,1536]{1,0:T(8,128)(2,1)} %all-gather.6.cloned.1.call-done, bf16[1536,1536]{1,0:T(8,128)(2,1)} %param.10), kind=kOutput, calls=%fused_computation.56 | convolution fusion | flops 2415919104 | bytes 9437184 | tf_op jit(solution)/shard_map/dot_general | solution.py:52
  69.2 21.7 %all-gather.8.cloned.1.call-done = bf16[512,1536]{1,0:T(8,128)(2,1)} async-done(((bf16[64,1536]{1,0:T(8,128)(2,1)}), bf16[512,1536]{1,0:T(8,128)(2,1)}) %all-gather.8.cloned.1.call-update) | async-done | bytes 1572880 | tf_op jit(solution)/shard_map/all_gather | solution.py:46
  90.9 4.9 %fusion.31 = f32[512,1536]{1,0:T(8,128)S(1)} fusion(bf16[512,1536]{1,0:T(8,128)(2,1)} %all-gather.8.cloned.1.call-done, bf16[1536,1536]{1,0:T(8,128)(2,1)} %param.10), kind=kOutput, calls=%fused_computation.57 | convolution fusion | flops 2415919104 | bytes 9437184 | tf_op jit(solution)/shard_map/dot_general | solution.py:53
  95.9 3.3 pad_maximum_fusion
  99.1 0.0 reduce-scatter.5.cloned.1.call-update
  99.1 0.0 all-gather.10.cloned.1.call-start
  99.2 38.2 %reduce-scatter.9.cloned.1.call-done = f32[128,1536]{1,0:T(8,128)} async-done(((f32[512,1536]{1,0:T(8,128)}), f32[128,1536]{1,0:T(8,128)}) %reduce-scatter.9.cloned.1.call-update) | async-done | bytes 786448 | tf_op jit(solution)/shard_map/reduce_scatter | solution.py:83
  137.4 73.5 %reduce-scatter.5.cloned.1.call-done = f32[128,3072]{1,0:T(8,128)} async-done(((f32[512,3072]{1,0:T(8,128)}), f32[128,3072]{1,0:T(8,128)}) %reduce-scatter.5.cloned.1.call-update) | async-done | bytes 1572880 | tf_op jit(solution)/shard_map/reduce_scatter | solution.py:49
  210.9 2.9 multiply_convert_fusion
  213.8 0.0 all-gather.14.cloned.1.call-start
  213.8 1.0 pad_maximum_fusion.1
  214.8 0.0 reduce-scatter.7.cloned.1.call-start
  214.9 29.9 %all-gather.10.cloned.1.call-done = bf16[512,1536]{1,0:T(8,128)(2,1)} async-done(((bf16[128,1536]{1,0:T(8,128)(2,1)}), bf16[512,1536]{1,0:T(8,128)(2,1)}) %all-gather.10.cloned.1.call-update) | async-done | bytes 1572880 | tf_op jit(solution)/shard_map/all_gather | solution.py:75
  244.8 7.1 %fusion.32 = f32[512,1536]{1,0:T(8,128)} fusion(bf16[512,1536]{1,0:T(8,128)(2,1)} %all-gather.10.cloned.1.call-done, bf16[1536,1536]{1,0:T(8,128)(2,1)} %param.11), kind=kOutput, calls=%fused_computation.58 | convolution fusion | flops 2415919104 | bytes 9437184 | tf_op jit(solution)/shard_map/dot_general | solution.py:74
  251.9 0.2 reduce-scatter.11.cloned.1.call-start
  252.1 38.9 %all-gather.14.cloned.1.call-done = bf16[512,3072]{1,0:T(8,128)(2,1)} async-done(((bf16[128,3072]{1,0:T(8,128)(2,1)}), bf16[512,3072]{1,0:T(8,128)(2,1)}) %all-gather.14.cloned.1.call-update) | async-done | bytes 3145744 | tf_op jit(solution)/shard_map/all_gather | solution.py:88
  291.1 7.2 %fusion.4 = f32[512,1536]{1,0:T(8,128)} fusion(bf16[1536,1536]{1,0:T(8,128)(2,1)} %param.10, bf16[512,3072]{1,0:T(8,128)(2,1)} %all-gather.14.cloned.1.call-done), kind=kOutput, calls=%fused_computation.9 | convolution fusion | flops 2415919104 | bytes 9437184 | tf_op jit(solution)/shard_map/dot_general | solution.py:25
  298.2 2.1 copy-done.5
  300.4 7.6 %multiply_reduce_fusion.1 = (f32[]{:T(128)}, f32[1536,1536]{1,0:T(8,128)}) fusion(bf16[512,1536]{1,0:T(8,128)(2,1)} %all-gather.8.cloned.1.call-done, bf16[512,3072]{1,0:T(8,128)(2,1)S(1)} %copy-done.5), kind=kOutput, calls=%fused_computation.1 | convolution fusion | flops 2420637696 | bytes 12582916 | tf_op jit(solution)/shard_map/dot_general | solution.py:25
  308.0 6.3 %multiply_reduce_fusion = (f32[]{:T(128)}, f32[1536,1536]{1,0:T(8,128)}) fusion(bf16[512,1536]{1,0:T(8,128)(2,1)S(1)} %copy-done.7, bf16[512,3072]{1,0:T(8,128)(2,1)S(1)} %copy-done.6), kind=kOutput, calls=%fused_computation | convolution fusion | flops 2420637696 | bytes 12582916 | tf_op jit(solution)/shard_map/dot_general | solution.py:25
  315.7 18.1 %reduce-scatter.7.cloned.1.call-done = f32[64,1536]{1,0:T(8,128)} async-done(((f32[512,1536]{1,0:T(8,128)}), f32[64,1536]{1,0:T(8,128)}) %reduce-scatter.7.cloned.1.call-update) | async-done | bytes 393232 | tf_op jit(solution)/shard_map/reduce_scatter | solution.py:79
  333.8 1.7 fusion.29
  335.5 40.3 %reduce-scatter.11.cloned.1.call-done = f32[64,1536]{1,0:T(8,128)} async-done(((f32[512,1536]{1,0:T(8,128)}), f32[64,1536]{1,0:T(8,128)}) %reduce-scatter.11.cloned.1.call-update) | async-done | bytes 393232 | tf_op jit(solution)/shard_map/reduce_scatter | solution.py:95
  375.8 1.4 fusion.23
  377.1 15.5 %psum.62 = f32[1536]{0:T(1024)S(1)} all-reduce(f32[1536]{0:T(1024)S(1)} %get-tuple-element.6), channel_id=1, replica_groups=mesh['row'=8,'col'=4] {'row'}, use_global_device_ids=true, to_apply=%region_19.0 | all-reduce | flops 1536 | bytes 12288 | tf_op jit(solution)/shard_map/psum | solution.py:107
  392.6 0.6 multiply_reduce_fusion.3
  393.2 9.8 %all-reduce = (f32[64]{0:T(128)S(1)}, f32[64]{0:T(128)S(1)}) all-reduce(f32[64]{0:T(128)S(1)} %get-tuple-element.7, f32[64]{0:T(128)S(1)} %get-tuple-element.8), channel_id=1, replica_groups=mesh['row'=8,'col'=4] {'col'}, use_global_device_ids=true, to_apply=%region_15.0 | all-reduce | flops 128 | bytes 1024 | tf_op jit(solution)/shard_map/psum | solution.py:99
  403.7 36.9 %psum.63 = f32[]{:T(128)} all-reduce(f32[]{:T(128)S(6)} %add.60), channel_id=1, replica_groups=mesh['row'=8,'col'=4] {'row','col'}, use_global_device_ids=true, to_apply=%region_21.0 | all-reduce | flops 1 | bytes 8 | tf_op jit(solution)/shard_map/psum | solution.py:109
  441.3 0.6 broadcast_multiply_fusion.2
  441.9 8.7 %broadcast_multiply_fusion = f32[1536,1536]{1,0:T(8,128)} fusion(f32[1536,1536]{1,0:T(8,128)} %get-tuple-element.31, f32[]{:T(128)S(6)} %min.3), kind=kLoop, calls=%fused_computation.3 | loop fusion | flops 2359296 | bytes 18874372 | tf_op jit(solution)/shard_map/mul | solution.py:114
  450.6 4.8 %broadcast_multiply_fusion.1 = f32[1536,1536]{1,0:T(8,128)} fusion(f32[1536,1536]{1,0:T(8,128)S(1)} %bitcast.12, f32[]{:T(128)S(6)} %min.3), kind=kLoop, calls=%fused_computation.4 | loop fusion | flops 2359296 | bytes 18874372 | tf_op jit(solution)/shard_map/mul | solution.py:114
  455.4 0.9 fusion.22
  (29 shorter events, 0.1 us)
Async XLA Ops:
  7.2 30.5 %all-gather.12.cloned.1.call-start = ((), (), s32[]{:S(2)}) async-start(), calls=%async_computation.9 | async-start | bytes 1769472 | tf_op jit(solution)/shard_map/all_gather | solution.py:82
  7.9 56.4 %all-gather.6.cloned.1.call-start = ((), (), s32[]{:S(2)}) async-start(), calls=%async_computation.4 | async-start | bytes 1769472 | tf_op jit(solution)/shard_map/all_gather | solution.py:45
  23.6 67.3 %all-gather.8.cloned.1.call-start = ((), (), s32[]{:S(2)}) async-start(), calls=%async_computation.5 | async-start | bytes 1769472 | tf_op jit(solution)/shard_map/all_gather | solution.py:46
  24.3 113.1 %reduce-scatter.9.cloned.1.call-start = ((), (), s32[]{:S(2)}) async-start(), calls=%async_computation.10 | async-start | bytes 3932160 | tf_op jit(solution)/shard_map/reduce_scatter | solution.py:83
  44.8 166.1 %reduce-scatter.5.cloned.1.call-start = ((), (), s32[]{:S(2)}) async-start(), calls=%async_computation.6 | async-start | bytes 7864320 | tf_op jit(solution)/shard_map/reduce_scatter | solution.py:49
  99.1 145.6 %all-gather.10.cloned.1.call-start = ((), (), s32[]{:S(2)}) async-start(), calls=%async_computation.7 | async-start | bytes 1966080 | tf_op jit(solution)/shard_map/all_gather | solution.py:75
  213.8 77.3 %all-gather.14.cloned.1.call-start = ((), (), s32[]{:S(2)}) async-start(), calls=%async_computation.11 | async-start | bytes 3932160 | tf_op jit(solution)/shard_map/all_gather | solution.py:88
  214.8 119.0 %reduce-scatter.7.cloned.1.call-start = ((), (), s32[]{:S(2)}) async-start(), calls=%async_computation.8 | async-start | bytes 3538944 | tf_op jit(solution)/shard_map/reduce_scatter | solution.py:79
  251.9 123.9 %reduce-scatter.11.cloned.1.call-start = ((), (), s32[]{:S(2)}) async-start(), calls=%async_computation.12 | async-start | bytes 3538944 | tf_op jit(solution)/shard_map/reduce_scatter | solution.py:95
  298.2 2.2 copy-start.5
  300.4 7.6 %copy-start.6 = (bf16[512,3072]{1,0:T(8,128)(2,1)S(1)}, bf16[512,3072]{1,0:T(8,128)(2,1)}, u32[]{:S(2)}) copy-start(bf16[512,3072]{1,0:T(8,128)(2,1)} %all-gather.14.cloned.1.call-done) | copy-start | bytes 9437188
  300.4 7.6 %copy-start.7 = (bf16[512,1536]{1,0:T(8,128)(2,1)S(1)}, bf16[512,1536]{1,0:T(8,128)(2,1)}, u32[]{:S(2)}) copy-start(bf16[512,1536]{1,0:T(8,128)(2,1)} %all-gather.12.cloned.1.call-done) | copy-start | bytes 4718596
  308.0 25.8 %copy-start.1 = (bf16[64,1536]{1,0:T(8,128)(2,1)S(1)}, bf16[64,1536]{1,0:T(8,128)(2,1)}, u32[]{:S(2)}) copy-start(bf16[64,1536]{1,0:T(8,128)(2,1)} %param.6) | copy-start | bytes 589828
  308.0 67.7 %copy-start = (bf16[64,1536]{1,0:T(8,128)(2,1)S(1)}, bf16[64,1536]{1,0:T(8,128)(2,1)}, u32[]{:S(2)}) copy-start(bf16[64,1536]{1,0:T(8,128)(2,1)} %param.7) | copy-start | bytes 589828
  308.0 67.7 %copy-start.4 = (f32[1536]{0:T(1024)S(1)}, f32[1536]{0:T(1024)}, u32[]{:S(2)}) copy-start(f32[1536]{0:T(1024)} %param.9) | copy-start | bytes 18436
  375.8 74.8 %slice-start = ((s8[9437184]{0:T(1024)(128)(4,1)}), s8[1048576]{0:T(1024)(128)(4,1)S(1)}, s32[]{:S(2)}) async-start(s8[9437184]{0:T(1024)(128)(4,1)} %bitcast.11), calls=%async_computation.13 | async-start | bytes 2097152
  441.9 8.7 %slice-start.1 = ((s8[9437184]{0:T(1024)(128)(4,1)}), s8[4194304]{0:T(1024)(128)(4,1)S(1)}, s32[]{:S(2)}) async-start(s8[9437184]{0:T(1024)(128)(4,1)} %bitcast.11), calls=%async_computation.14 | async-start | bytes 8388608
  441.9 8.7 %slice-start.2 = ((s8[9437184]{0:T(1024)(128)(4,1)}), s8[4194304]{0:T(1024)(128)(4,1)S(1)}, s32[]{:S(2)}) async-start(s8[9437184]{0:T(1024)(128)(4,1)} %bitcast.11), calls=%async_computation.15 | async-start | bytes 8388608
  450.6 4.8 %copy-start.2 = (f32[64,1536]{1,0:T(8,128)S(1)}, f32[64,1536]{1,0:T(8,128)}, u32[]{:S(2)}) copy-start(f32[64,1536]{1,0:T(8,128)} %reduce-scatter.11.cloned.1.call-done) | copy-start | bytes 1179652
  450.6 4.8 %copy-start.3 = (bf16[64,1536]{1,0:T(8,128)(2,1)S(1)}, bf16[64,1536]{1,0:T(8,128)(2,1)}, u32[]{:S(2)}) copy-start(bf16[64,1536]{1,0:T(8,128)(2,1)} %param.8) | copy-start | bytes 589828
Sparse Core Ops, SparseCore 0:
  9.6 27.9 all-gather.11
  39.8 24.3 all-gather.5
  66.5 24.3 all-gather.7
  94.3 43.0 reduce-scatter.8
  140.8 70.0 reduce-scatter.4
  213.9 30.8 all-gather.9
  247.2 43.8 all-gather.13
  293.4 40.3 reduce-scatter.6
  336.1 39.6 reduce-scatter.10
